TPU v7x, 128 devices: a whole 4x4x4 slice. The times are simulated.
128 devices in a mesh: gx: 16 (over z, y), gy: 8 (over x, core).
Axes of the slice: x: 4, y: 4, z: 4, core: 2. Of those that a mesh axis runs over, the one named last changes fastest.
Arguments:
- velocity_u: float32 [4, 2560, 2048], P(None, 'gy', 'gx'), may hold values from -6 to 6
- velocity_v: float32 [4, 2560, 2048], P(None, 'gy', 'gx'), may hold values from -6 to 6
- tracer: float32 [4, 2560, 2048], P(None, 'gy', 'gx'), may hold values from -6 to 6
- pressure_old: float32 [2560, 2048], P('gy', 'gx'), may hold values from -6 to 6
- depth: float32 [2560, 2048], P('gy', 'gx'), may hold values from 0.5 to 2
- helm: float32 [2560, 2048], P('gy', 'gx'), may hold values from 0.05 to 0.5
- land_mask: int32 [2560, 2048], P('gy', 'gx'), may hold values from 0 to 1, as said below
- clinic_map: int32 [64, 16], replicated, may hold values from 0 to 1, as said below
- tropic_map: int32 [64, 16], replicated, may hold values from -1 to 95, as said below
Outputs:
- velocity_u_new: float32 [4, 2560, 2048], P(None, 'gy', 'gx')
- velocity_v_new: float32 [4, 2560, 2048], P(None, 'gy', 'gx')
- tracer_new: float32 [4, 2560, 2048], P(None, 'gy', 'gx')
- pressure: float32 [2560, 2048], P('gy', 'gx')
Inputs may be any that keep to these rules, and one draw needn't show every extreme that they name: `land_mask`: rows 0 and 2559 are land; every column of a block whose tropic_map entry is -1 is land; every other block has an ocean column. `clinic_map`: 1 exactly on the blocks whose tropic_map entry is not -1. `tropic_map`: A quarter of the blocks of every device's clinic domain are -1. Another value t places the block in slot t % 6 of the device with gx index t // 6 and the gy index of the device that holds the block's rows; no slot is named twice. The blocks of one device's clinic domain place at most 1 block on any one device, and this bound is reached; every device receives at most 6 blocks, and this bound is reached.
All inputs are finite; a program needn't handle non-finite values.
Results may differ from a plain program's by a relative error of at most 0.00026.
Values sent between devices are 32-bit elements; how exact they have to be, the bound alone decides.
A program may use at most 64 MiB of HBM per device.

v0:
```python
import jax
import jax.numpy as jnp
from jax import lax
from jax.sharding import Mesh
from jax.sharding import PartitionSpec as P

BX = 128
BY = 40
ITERS = 4
GX_GY = ("gx_0", "gx_1", "gy_0", "gy_1")
GY = ("gy_0", "gy_1")
GX = ("gx_0", "gx_1")
step_time = 0.2
viscosity = 0.5
diffusivity = 0.5
vertical = 0.5
gravity = 1.0


def one_axis_at_a_time(x, axes):
    for axis in axes:
        x = lax.psum(x, axis)
    return x


def padded_2(cells, sides, width):
    for axis, dim in sides:
        count = lax.axis_size(axis)
        head = lax.slice_in_dim(cells, 0, width, axis=dim)
        tail = lax.slice_in_dim(cells, cells.shape[dim] - width, cells.shape[dim], axis=dim)
        cells = jnp.concatenate(
            [
                lax.ppermute(tail, axis, [(i, (i + 1) % count) for i in range(count)]),
                cells,
                lax.ppermute(head, axis, [((i + 1) % count, i) for i in range(count)]),
            ],
            axis=dim,
        )
    return cells


def padded_3(x, sides, width):
    edges = {}
    for axis, dim in sides:
        size, length = (lax.axis_size(axis), x.shape[dim])
        up = [(i, (i + 1) % size) for i in range(size)]
        last = lax.slice_in_dim(x, length - width, length, axis=dim)
        first = lax.slice_in_dim(x, 0, width, axis=dim)
        edges[dim] = (
            lax.ppermute(last, axis, up),
            lax.ppermute(first, axis, [(b, a) for a, b in up]),
        )
    done = []
    for _, dim in sides:
        low, high = edges[dim]
        around = [(width, width) if d in done else (0, 0) for d in range(x.ndim)]
        x = jnp.concatenate([jnp.pad(low, around), x, jnp.pad(high, around)], axis=dim)
        done.append(dim)
    return x


def beside_all(padded):
    centre = padded[..., 1:-1, 1:-1]
    return (
        centre,
        padded[..., 1:-1, 2:],
        padded[..., 1:-1, :-2],
        padded[..., 2:, 1:-1],
        padded[..., :-2, 1:-1],
    )


def faces(depths):
    centre, east_v, west_v, north_v, south_v = beside_all(depths)
    return (
        jnp.minimum(centre, east_v),
        jnp.minimum(centre, west_v),
        jnp.minimum(centre, north_v),
        jnp.minimum(centre, south_v),
    )


def diffuse(padded, coeffs):
    centre, east_v, west_v, north_v, south_v = beside_all(padded)
    face_e, face_w, face_n, face_s = coeffs
    return (
        face_e * (east_v - centre)
        + face_w * (west_v - centre)
        + face_n * (north_v - centre)
        + face_s * (south_v - centre)
    )


def mixing(field):
    diff = field[1:] - field[:-1]
    zero = jnp.zeros_like(field[:1])
    return jnp.concatenate([diff, zero], 0) - jnp.concatenate([zero, diff], 0)


def pair_totals(residual, precond, image):
    return (
        one_axis_at_a_time(jnp.sum(residual * precond), GX_GY),
        one_axis_at_a_time(jnp.sum(precond * image), GX_GY),
    )


def conjugate(apply, rhs, start, diagonal):
    solution = start
    residual = rhs - apply(start)
    precond = residual / diagonal
    image = apply(precond)
    rz_now, curve = pair_totals(residual, precond, image)
    alpha = rz_now / curve
    direction = precond
    along = image
    for step in range(ITERS):
        solution = solution + alpha * direction
        residual = residual - alpha * along
        if step + 1 < ITERS:
            precond = residual / diagonal
            image = apply(precond)
            rz_next, curve = pair_totals(residual, precond, image)
            ratio = rz_next / rz_now
            alpha = rz_next / (curve - ratio * rz_next / alpha)
            direction = precond + ratio * direction
            along = image + ratio * along
            rz_now = rz_next
    return solution


def on_device(
    velocity_u, velocity_v, tracer, pressure_old, depth, helm, land_mask, clinic_map, tropic_map
):
    f32 = jnp.float32
    levels, rows, cols = velocity_u.shape
    width_y = lax.axis_size(GY)
    col_dev = lax.axis_index(GX)
    row_dev = lax.axis_index(GY)
    per_y = rows // BY
    per_x = cols // BX
    total_rows = rows * width_y
    my_tropic = lax.dynamic_slice(tropic_map, (row_dev * per_y, col_dev * per_x), (per_y, per_x))
    my_clinic = lax.dynamic_slice(clinic_map, (row_dev * per_y, col_dev * per_x), (per_y, per_x))

    def spread(blockwise):
        return jnp.broadcast_to(blockwise[:, None, :, None], (per_y, BY, per_x, BX)).reshape(
            rows, cols
        )

    ocean = land_mask.astype(f32)
    domain = spread((my_tropic >= 0).astype(f32))
    active = spread(my_clinic.astype(f32))
    solve_mask = ocean * domain
    wet = depth * solve_mask
    stacked = jnp.concatenate([velocity_u, velocity_v, tracer, wet[None]], 0)
    padded = padded_2(stacked, ((GX, 2), (GY, 1)), 2)
    u_pad = padded[:levels]
    v_pad = padded[levels : 2 * levels]
    wet_pad = padded[3 * levels]
    cycle_faces = faces(wet_pad)
    inner_faces = tuple((face[1:-1, 1:-1] for face in cycle_faces))
    latitude = ((row_dev * rows - 1 + jnp.arange(rows + 2)) % total_rows).astype(f32)
    coriolis = (0.2 + 0.6 * ((latitude + 0.5) / total_rows)).reshape(rows + 2, 1)
    u_cycle = u_pad[:, 1:-1, 1:-1]
    v_cycle = v_pad[:, 1:-1, 1:-1]
    u_star = u_cycle + step_time * (
        vertical * mixing(u_cycle) + viscosity * diffuse(u_pad, cycle_faces) + coriolis * v_cycle
    )
    v_star = v_cycle + step_time * (
        vertical * mixing(v_cycle) + viscosity * diffuse(v_pad, cycle_faces) - coriolis * u_cycle
    )
    tracer_pad = padded[2 * levels : 3 * levels, 1:-1, 1:-1]
    _, tracer_e, tracer_w, tracer_n, tracer_s = beside_all(tracer_pad)
    tracer_raw = tracer + step_time * (
        vertical * mixing(tracer)
        + diffusivity * diffuse(tracer_pad, inner_faces)
        - 0.5 * (velocity_u * (tracer_e - tracer_w) + velocity_v * (tracer_n - tracer_s))
    )
    thick = ((2 * jnp.arange(levels) + 1).astype(f32) / (levels * levels)).reshape(levels, 1, 1)
    wet_cycle = wet_pad[1:-1, 1:-1]
    east_flow = wet_cycle * jnp.sum(thick * u_star, 0)
    north_flow = wet_cycle * jnp.sum(thick * v_star, 0)
    forcing = solve_mask * (
        -(east_flow[1:-1, 1:-1] - east_flow[1:-1, :-2])
        - (north_flow[1:-1, 1:-1] - north_flow[:-2, 1:-1])
    )
    face_e, face_w, face_n, face_s = inner_faces
    diagonal = helm + face_e + face_w + face_n + face_s
    start = solve_mask * pressure_old

    def plane_pad(field):
        return padded_3(field, ((GX, 1), (GY, 0)), 1)

    def apply_plane(field):
        _, east_v, west_v, north_v, south_v = beside_all(plane_pad(field))
        return (
            diagonal * field
            - face_e * east_v
            - face_w * west_v
            - face_n * north_v
            - face_s * south_v
        )

    pressure = conjugate(apply_plane, forcing, start, diagonal)
    _, east_p, _, north_p, _ = beside_all(plane_pad(pressure))
    grad_x = east_p - pressure
    grad_y = north_p - pressure
    keep_mask = active * ocean
    u_new = keep_mask * (u_star[:, 1:-1, 1:-1] - gravity * grad_x) + (1.0 - active) * velocity_u
    v_new = keep_mask * (v_star[:, 1:-1, 1:-1] - gravity * grad_y) + (1.0 - active) * velocity_v
    t_new = keep_mask * tracer_raw + (1.0 - active) * tracer
    return (u_new, v_new, t_new, pressure)


def solution(mesh):
    split = Mesh(mesh.devices.reshape(4, 4, 4, 2), ("gx_0", "gx_1", "gy_0", "gy_1"))
    in_specs = (
        P(None, GY, GX),
        P(None, GY, GX),
        P(None, GY, GX),
        P(GY, GX),
        P(GY, GX),
        P(GY, GX),
        P(GY, GX),
        P(),
        P(),
    )
    out_specs = (P(None, GY, GX), P(None, GY, GX), P(None, GY, GX), P(GY, GX))
    return jax.shard_map(
        on_device, mesh=split, in_specs=in_specs, out_specs=out_specs, check_vma=False
    )
```

profile of v0, /device:TPU:0, one launch (start us, length us, event | category | flops | bytes accessed | tf_op | source)
XLA Modules:
  0.0 265.8 jit_solution(10132375841164672830)
XLA Ops:
  0.6 1.1 copy.47
  1.8 1.0 copy.36
  3.8 1.0 copy.37
  5.8 1.4 copy.40
  7.4 1.4 copy.38
  9.5 6.7 %collective-permute-start.1 = (f32[13,320,2]{1,2,0:T(2,128)S(1)}, f32[13,320,2]{1,2,0:T(2,128)S(1)}, u32[]{:S(2)}, u32[]{:S(2)}) collective-permute-start(f32[13,320,2]{1,2,0:T(2,128)S(1)} %get-tuple-element.73), channel_id=1, source_target_pairs={{8,0},{16,8},{24,16},{32,24},{40,32},{48,40},{56,48},{64,56},{72,6... | collective-permute-start | bytes 99848 | tf_op jit(solution)/shard_map/ppermute | solution.py:35
  16.8 5.3 %collective-permute-start.4 = (f32[320,1]{0,1:T(1,128)}, f32[320,1]{0,1:T(1,128)}, u32[]{:S(2)}, u32[]{:S(2)}) collective-permute-start(f32[320,1]{0,1:T(1,128)} %get-tuple-element.108), channel_id=1, source_target_pairs={{8,0},{16,8},{24,16},{32,24},{40,32},{48,40},{56,48},{64,56},{72,6... | collective-permute-start | bytes 3848 | tf_op jit(solution)/shard_map/ppermute | solution.py:51
  23.5 1.3 pad_maximum_fusion.6
  24.8 2.3 copy.42
  27.1 2.3 collective-permute-start.3
  29.4 1.1 copy.41
  31.1 1.7 copy.48
  32.8 3.0 %collective-permute-start.6 = (f32[1,128]{0,1:T(8,128)}, f32[1,128]{0,1:T(8,128)}, u32[]{:S(2)}, u32[]{:S(2)}) collective-permute-start(f32[1,128]{0,1:T(8,128)} %get-tuple-element.105), channel_id=1, source_target_pairs={{1,0},{2,1},{3,2},{4,3},{5,4},{6,5},{7,6},{0,7},{9,8},{10,9},{11,1... | collective-permute-start | bytes 1544 | tf_op jit(solution)/shard_map/ppermute | solution.py:51
  35.8 1.1 copy.44
  36.9 2.0 copy.43
  38.9 2.3 pad_maximum_fusion
  42.5 8.3 %multiply_reduce_fusion.1 = (f32[322,130]{0,1:T(8,128)S(1)}, f32[322,130]{0,1:T(8,128)S(1)}, f32[4,322,130]{1,2,0:T(8,128)}, f32[4,322,130]{1,2,0:T(8,128)}) fusion(f32[4]{0:T(128)S(1)} %copy-done.28, f32[13,324,132]{1,2,0:T(8,128)S(1)} %pad_maximum_fusion, f32[322]{0:T(512)S(1)} %fusion.91, f32[13,320,2]{1,2,0:T(2,128)S(1)} %collective-permute-done.1, ...), kind=kLoop, calls=%fused_computation.40 | loop fusion | flops 10632440 | bytes 9592600 | tf_op jit(solution)/shard_map/reduce_sum | solution.py:181
  51.0 1.5 fusion.102
  52.5 5.4 %collective-permute-start.8 = (f32[320,1]{0,1:T(1,128)S(1)}, f32[320,1]{0,1:T(1,128)S(1)}, u32[]{:S(2)}, u32[]{:S(2)}) collective-permute-start(f32[320,1]{0,1:T(1,128)S(1)} %get-tuple-element.104), channel_id=1, source_target_pairs={{8,0},{16,8},{24,16},{32,24},{40,32},{48,40},{56,48},{64,56},{72,6... | collective-permute-start | bytes 3848 | tf_op jit(solution)/shard_map/ppermute | solution.py:51
  58.0 3.0 %collective-permute-start.10 = (f32[1,128]{0,1:T(8,128)S(1)}, f32[1,128]{0,1:T(8,128)S(1)}, u32[]{:S(2)}, u32[]{:S(2)}) collective-permute-start(f32[1,128]{0,1:T(8,128)S(1)} %get-tuple-element.101), channel_id=1, source_target_pairs={{1,0},{2,1},{3,2},{4,3},{5,4},{6,5},{7,6},{0,7},{9,8},{10,9},{11,1... | collective-permute-start | bytes 1544 | tf_op jit(solution)/shard_map/ppermute | solution.py:51
  61.0 1.9 collective-permute-done.11
  62.9 1.9 collective-permute-done.9
  64.9 1.7 multiply_reduce_fusion.7
  66.6 8.4 %all-reduce.28 = (f32[]{:T(128)}, f32[]{:T(128)}) all-reduce(f32[]{:T(128)} %get-tuple-element.19, f32[]{:T(128)} %get-tuple-element.18), channel_id=1, replica_groups=mesh['gx_0'=4,'gx_1'=4,'gy_0'=4,'gy_1'=2] {'gx_0'}, use_global_device_ids=true, to_apply=%region_3.4 | all-reduce | flops 2 | bytes 16 | tf_op jit(solution)/shard_map/psum | solution.py:22
  75.0 12.4 %all-reduce.24 = (f32[]{:T(128)}, f32[]{:T(128)}) all-reduce(f32[]{:T(128)} %get-tuple-element.44, f32[]{:T(128)} %get-tuple-element.45), channel_id=1, replica_groups=mesh['gx_0'=4,'gx_1'=4,'gy_0'=4,'gy_1'=2] {'gx_1'}, use_global_device_ids=true, to_apply=%region_4.5 | all-reduce | flops 2 | bytes 16 | tf_op jit(solution)/shard_map/psum | solution.py:22
  87.3 8.4 %all-reduce.20 = (f32[]{:T(128)}, f32[]{:T(128)}) all-reduce(f32[]{:T(128)} %get-tuple-element.36, f32[]{:T(128)} %get-tuple-element.37), channel_id=1, replica_groups=mesh['gx_0'=4,'gx_1'=4,'gy_0'=4,'gy_1'=2] {'gy_0'}, use_global_device_ids=true, to_apply=%region_5.6 | all-reduce | flops 2 | bytes 16 | tf_op jit(solution)/shard_map/psum | solution.py:22
  95.7 3.1 %all-reduce.32 = (f32[]{:T(128)}, f32[]{:T(128)}) all-reduce(f32[]{:T(128)} %get-tuple-element.28, f32[]{:T(128)} %get-tuple-element.29), channel_id=1, replica_groups=mesh['gx_0'=4,'gx_1'=4,'gy_0'=4,'gy_1'=2] {'gy_1'}, use_global_device_ids=true, to_apply=%region_6.7 | all-reduce | flops 2 | bytes 16 | tf_op jit(solution)/shard_map/psum | solution.py:22
  100.1 1.1 fusion.100
  101.3 2.0 collective-permute-start.13
  103.4 3.0 %collective-permute-start.14 = (f32[1,128]{0,1:T(8,128)S(1)}, f32[1,128]{0,1:T(8,128)S(1)}, u32[]{:S(2)}, u32[]{:S(2)}) collective-permute-start(f32[1,128]{0,1:T(8,128)S(1)} %get-tuple-element.97), channel_id=1, source_target_pairs={{1,0},{2,1},{3,2},{4,3},{5,4},{6,5},{7,6},{0,7},{9,8},{10,9},{11,1... | collective-permute-start | bytes 1544 | tf_op jit(solution)/shard_map/ppermute | solution.py:51
  106.3 1.9 collective-permute-done.15
  108.3 3.0 %multiply_reduce_fusion.5 = (f32[]{:T(128)}, f32[]{:T(128)}, f32[320,128]{0,1:T(8,128)}) fusion(f32[320,128]{0,1:T(8,128)S(1)} %get-tuple-element.60, f32[320,128]{0,1:T(8,128)S(1)} %get-tuple-element.61, f32[320,1]{0,1:T(1,128)S(1)} %collective-permute-done.12, f32[320,1]{0,1:T(1,128)S(1)} %collective-permute-done.13, ...), kind=kLoop, calls=%fused_computation.190 | loop fusion | flops 1105918 | bytes 1314312 | tf_op jit(solution)/shard_map/reduce_sum | solution.py:103
  111.3 8.4 %all-reduce.27 = (f32[]{:T(128)}, f32[]{:T(128)}) all-reduce(f32[]{:T(128)} %get-tuple-element.17, f32[]{:T(128)} %get-tuple-element.16), channel_id=1, replica_groups=mesh['gx_0'=4,'gx_1'=4,'gy_0'=4,'gy_1'=2] {'gx_0'}, use_global_device_ids=true, to_apply=%region_13.14 | all-reduce | flops 2 | bytes 16 | tf_op jit(solution)/shard_map/psum | solution.py:22
  119.7 12.4 %all-reduce.23 = (f32[]{:T(128)}, f32[]{:T(128)}) all-reduce(f32[]{:T(128)} %get-tuple-element.42, f32[]{:T(128)} %get-tuple-element.43), channel_id=1, replica_groups=mesh['gx_0'=4,'gx_1'=4,'gy_0'=4,'gy_1'=2] {'gx_1'}, use_global_device_ids=true, to_apply=%region_14.15 | all-reduce | flops 2 | bytes 16 | tf_op jit(solution)/shard_map/psum | solution.py:22
  132.1 9.2 %all-reduce.19 = (f32[]{:T(128)}, f32[]{:T(128)}) all-reduce(f32[]{:T(128)} %get-tuple-element.34, f32[]{:T(128)} %get-tuple-element.35), channel_id=1, replica_groups=mesh['gx_0'=4,'gx_1'=4,'gy_0'=4,'gy_1'=2] {'gy_0'}, use_global_device_ids=true, to_apply=%region_15.16 | all-reduce | flops 2 | bytes 16 | tf_op jit(solution)/shard_map/psum | solution.py:22
  141.3 3.1 %all-reduce.31 = (f32[]{:T(128)}, f32[]{:T(128)}) all-reduce(f32[]{:T(128)} %get-tuple-element.26, f32[]{:T(128)} %get-tuple-element.27), channel_id=1, replica_groups=mesh['gx_0'=4,'gx_1'=4,'gy_0'=4,'gy_1'=2] {'gy_1'}, use_global_device_ids=true, to_apply=%region_16.17 | all-reduce | flops 2 | bytes 16 | tf_op jit(solution)/shard_map/psum | solution.py:22
  148.9 1.2 fusion.98
  151.0 1.4 collective-permute-start.17
  152.3 3.0 %collective-permute-start.18 = (f32[1,128]{0,1:T(8,128)S(1)}, f32[1,128]{0,1:T(8,128)S(1)}, u32[]{:S(2)}, u32[]{:S(2)}) collective-permute-start(f32[1,128]{0,1:T(8,128)S(1)} %get-tuple-element.93), channel_id=1, source_target_pairs={{1,0},{2,1},{3,2},{4,3},{5,4},{6,5},{7,6},{0,7},{9,8},{10,9},{11,1... | collective-permute-start | bytes 1544 | tf_op jit(solution)/shard_map/ppermute | solution.py:51
  156.1 1.1 collective-permute-done.19
  157.9 1.7 multiply_reduce_fusion.3
  159.6 8.4 %all-reduce.26 = (f32[]{:T(128)}, f32[]{:T(128)}) all-reduce(f32[]{:T(128)} %get-tuple-element.15, f32[]{:T(128)} %get-tuple-element.14), channel_id=1, replica_groups=mesh['gx_0'=4,'gx_1'=4,'gy_0'=4,'gy_1'=2] {'gx_0'}, use_global_device_ids=true, to_apply=%region_23.24 | all-reduce | flops 2 | bytes 16 | tf_op jit(solution)/shard_map/psum | solution.py:22
  168.0 12.3 %all-reduce.22 = (f32[]{:T(128)}, f32[]{:T(128)}) all-reduce(f32[]{:T(128)} %get-tuple-element.40, f32[]{:T(128)} %get-tuple-element.41), channel_id=1, replica_groups=mesh['gx_0'=4,'gx_1'=4,'gy_0'=4,'gy_1'=2] {'gx_1'}, use_global_device_ids=true, to_apply=%region_24.25 | all-reduce | flops 2 | bytes 16 | tf_op jit(solution)/shard_map/psum | solution.py:22
  180.3 8.4 %all-reduce.18 = (f32[]{:T(128)}, f32[]{:T(128)}) all-reduce(f32[]{:T(128)} %get-tuple-element.32, f32[]{:T(128)} %get-tuple-element.33), channel_id=1, replica_groups=mesh['gx_0'=4,'gx_1'=4,'gy_0'=4,'gy_1'=2] {'gy_0'}, use_global_device_ids=true, to_apply=%region_25.26 | all-reduce | flops 2 | bytes 16 | tf_op jit(solution)/shard_map/psum | solution.py:22
  188.7 3.1 %all-reduce.30 = (f32[]{:T(128)}, f32[]{:T(128)}) all-reduce(f32[]{:T(128)} %get-tuple-element.24, f32[]{:T(128)} %get-tuple-element.25), channel_id=1, replica_groups=mesh['gx_0'=4,'gx_1'=4,'gy_0'=4,'gy_1'=2] {'gy_1'}, use_global_device_ids=true, to_apply=%region_26.27 | all-reduce | flops 2 | bytes 16 | tf_op jit(solution)/shard_map/psum | solution.py:22
  195.7 1.4 fusion.96
  197.5 1.9 collective-permute-start.21
  199.4 2.2 collective-permute-start.22
  201.6 1.7 slice.428
  203.4 1.7 slice.427
  205.1 1.7 slice.426
  207.7 1.0 fusion.35
  208.7 8.3 %all-reduce.25 = (f32[]{:T(128)}, f32[]{:T(128)}) all-reduce(f32[]{:T(128)} %get-tuple-element.13, f32[]{:T(128)} %get-tuple-element.12), channel_id=1, replica_groups=mesh['gx_0'=4,'gx_1'=4,'gy_0'=4,'gy_1'=2] {'gx_0'}, use_global_device_ids=true, to_apply=%region_33.34 | all-reduce | flops 2 | bytes 16 | tf_op jit(solution)/shard_map/psum | solution.py:22
  217.1 12.5 %all-reduce.21 = (f32[]{:T(128)}, f32[]{:T(128)}) all-reduce(f32[]{:T(128)} %get-tuple-element.38, f32[]{:T(128)} %get-tuple-element.39), channel_id=1, replica_groups=mesh['gx_0'=4,'gx_1'=4,'gy_0'=4,'gy_1'=2] {'gx_1'}, use_global_device_ids=true, to_apply=%region_34.35 | all-reduce | flops 2 | bytes 16 | tf_op jit(solution)/shard_map/psum | solution.py:22
  229.6 9.1 %all-reduce.17 = (f32[]{:T(128)}, f32[]{:T(128)}) all-reduce(f32[]{:T(128)} %get-tuple-element.30, f32[]{:T(128)} %get-tuple-element.31), channel_id=1, replica_groups=mesh['gx_0'=4,'gx_1'=4,'gy_0'=4,'gy_1'=2] {'gy_0'}, use_global_device_ids=true, to_apply=%region_35.36 | all-reduce | flops 2 | bytes 16 | tf_op jit(solution)/shard_map/psum | solution.py:22
  238.7 3.1 %all-reduce.29 = (f32[]{:T(128)}, f32[]{:T(128)}) all-reduce(f32[]{:T(128)} %get-tuple-element.22, f32[]{:T(128)} %get-tuple-element.23), channel_id=1, replica_groups=mesh['gx_0'=4,'gx_1'=4,'gy_0'=4,'gy_1'=2] {'gy_1'}, use_global_device_ids=true, to_apply=%region_36.37 | all-reduce | flops 2 | bytes 16 | tf_op jit(solution)/shard_map/psum | solution.py:22
  245.7 1.4 multiply_add_fusion.1
  248.3 1.0 collective-permute-start.26
  249.3 2.0 collective-permute-start.25
  251.3 4.4 %multiply_add_fusion = f32[4,320,128]{1,2,0:T(8,128)} fusion(f32[4,320,128]{1,2,0:T(8,128)S(1)} %copy.40, f32[4,320,128]{1,2,0:T(8,128)S(1)} %copy.39, f32[4,320,128]{1,2,0:T(8,128)S(1)} %copy.38, f32[13,320,2]{1,2,0:T(2,128)S(1)} %collective-permute-done.1, f32[1,320,128]{1,2,0:T(8,128)} %copy-done.13, f32[13,320,2]{1,2,0:T(2,128)S(1)} %collective-permute-done, ...), kind=kLoop, calls=%fused_computation.67 | loop fusion | flops 7536640 | bytes 4191296 | tf_op jit(solution)/shard_map/add | solution.py:211
  255.7 2.3 copy.63
  259.8 2.6 fusion.25
  262.5 2.2 copy.61
  264.7 1.1 copy.62
  (126 shorter events, 13.6 us)
Async XLA Ops:
  0.6 6.5 %copy-start.27 = (f32[4,320,128]{2,1,0:T(8,128)S(1)}, f32[4,320,128]{2,1,0:T(8,128)}, u32[]{:S(2)}) copy-start(f32[4,320,128]{2,1,0:T(8,128)} %param.10) | copy-start | bytes 1966084
  2.8 6.7 %copy-start.22 = (s32[320,128]{0,1:T(8,128)}, s32[320,128]{0,1:T(8,128)S(1)}, u32[]{:S(2)}) copy-start(s32[320,128]{0,1:T(8,128)S(1)} %copy.36) | copy-start | bytes 491524
  9.5 12.7 %copy-start.16 = (f32[320,128]{0,1:T(8,128)}, f32[320,128]{0,1:T(8,128)S(1)}, u32[]{:S(2)}) copy-start(f32[320,128]{0,1:T(8,128)S(1)} %get-tuple-element.82) | copy-start | bytes 491524
  9.5 32.9 %copy-start.13 = (f32[1,320,128]{1,2,0:T(8,128)}, f32[1,320,128]{1,2,0:T(8,128)S(1)}, u32[]{:S(2)}) copy-start(f32[1,320,128]{1,2,0:T(8,128)S(1)} %get-tuple-element.83) | copy-start | bytes 491524
  9.5 13.3 %collective-permute-start.1 = (f32[13,320,2]{1,2,0:T(2,128)S(1)}, f32[13,320,2]{1,2,0:T(2,128)S(1)}, u32[]{:S(2)}, u32[]{:S(2)}) collective-permute-start(f32[13,320,2]{1,2,0:T(2,128)S(1)} %get-tuple-element.73), channel_id=1, source_target_pairs={{8,0},{16,8},{24,16},{32,24},{40,32},{48,40},{56,48},{64,56},{72,6... | collective-permute-start | bytes 99848 | tf_op jit(solution)/shard_map/ppermute | solution.py:35
  16.2 7.3 %collective-permute-start = (f32[13,320,2]{1,2,0:T(2,128)S(1)}, f32[13,320,2]{1,2,0:T(2,128)S(1)}, u32[]{:S(2)}, u32[]{:S(2)}) collective-permute-start(f32[13,320,2]{1,2,0:T(2,128)S(1)} %get-tuple-element.72), channel_id=1, source_target_pairs={{0,8},{8,16},{16,24},{24,32},{32,40},{40,48},{48,56},{56,64},{64,7... | collective-permute-start | bytes 99848 | tf_op jit(solution)/shard_map/ppermute | solution.py:33
  16.8 34.2 %collective-permute-start.4 = (f32[320,1]{0,1:T(1,128)}, f32[320,1]{0,1:T(1,128)}, u32[]{:S(2)}, u32[]{:S(2)}) collective-permute-start(f32[320,1]{0,1:T(1,128)} %get-tuple-element.108), channel_id=1, source_target_pairs={{8,0},{16,8},{24,16},{32,24},{40,32},{48,40},{56,48},{64,56},{72,6... | collective-permute-start | bytes 3848 | tf_op jit(solution)/shard_map/ppermute | solution.py:51
  22.1 28.8 %collective-permute-start.5 = (f32[320,1]{0,1:T(1,128)}, f32[320,1]{0,1:T(1,128)}, u32[]{:S(2)}, u32[]{:S(2)}) collective-permute-start(f32[320,1]{0,1:T(1,128)} %get-tuple-element.107), channel_id=1, source_target_pairs={{0,8},{8,16},{16,24},{24,32},{32,40},{40,48},{48,56},{56,64},{64,7... | collective-permute-start | bytes 3848 | tf_op jit(solution)/shard_map/ppermute | solution.py:50
  22.9 28.1 %collective-permute-start.7 = (f32[1,128]{0,1:T(8,128)}, f32[1,128]{0,1:T(8,128)}, u32[]{:S(2)}, u32[]{:S(2)}) collective-permute-start(f32[1,128]{0,1:T(8,128)} %get-tuple-element.106), channel_id=1, source_target_pairs={{0,1},{1,2},{2,3},{3,4},{4,5},{5,6},{6,7},{7,0},{8,9},{9,10},{10,1... | collective-permute-start | bytes 1544 | tf_op jit(solution)/shard_map/ppermute | solution.py:50
  27.1 5.8 %collective-permute-start.3 = (f32[13,2,132]{2,1,0:T(2,128)}, f32[13,2,132]{2,1,0:T(2,128)}, u32[]{:S(2)}, u32[]{:S(2)}) collective-permute-start(f32[13,2,132]{2,1,0:T(2,128)} %copy.42), channel_id=1, source_target_pairs={{1,0},{2,1},{3,2},{4,3},{5,4},{6,5},{7,6},{0,7},{9,8},{10,9},{11,1... | collective-permute-start | bytes 41192 | tf_op jit(solution)/shard_map/ppermute | solution.py:35
  30.5 6.4 %collective-permute-start.2 = (f32[13,2,132]{2,1,0:T(2,128)}, f32[13,2,132]{2,1,0:T(2,128)}, u32[]{:S(2)}, u32[]{:S(2)}) collective-permute-start(f32[13,2,132]{2,1,0:T(2,128)} %copy.41), channel_id=1, source_target_pairs={{0,1},{1,2},{2,3},{3,4},{4,5},{5,6},{6,7},{7,0},{8,9},{9,10},{10,1... | collective-permute-start | bytes 41192 | tf_op jit(solution)/shard_map/ppermute | solution.py:33
  32.8 18.1 %collective-permute-start.6 = (f32[1,128]{0,1:T(8,128)}, f32[1,128]{0,1:T(8,128)}, u32[]{:S(2)}, u32[]{:S(2)}) collective-permute-start(f32[1,128]{0,1:T(8,128)} %get-tuple-element.105), channel_id=1, source_target_pairs={{1,0},{2,1},{3,2},{4,3},{5,4},{6,5},{7,6},{0,7},{9,8},{10,9},{11,1... | collective-permute-start | bytes 1544 | tf_op jit(solution)/shard_map/ppermute | solution.py:51
  41.3 1.2 copy-start
  41.3 1.2 copy-start.28
  42.4 22.5 %copy-start.1 = (f32[322,130]{0,1:T(8,128)}, f32[322,130]{0,1:T(8,128)S(1)}, u32[]{:S(2)}) copy-start(f32[322,130]{0,1:T(8,128)S(1)} %get-tuple-element.76) | copy-start | bytes 502324
  42.4 22.5 %copy-start.4 = (f32[322,130]{0,1:T(8,128)}, f32[322,130]{0,1:T(8,128)S(1)}, u32[]{:S(2)}) copy-start(f32[322,130]{0,1:T(8,128)S(1)} %get-tuple-element.77) | copy-start | bytes 502324
  42.4 22.5 %copy-start.7 = (f32[322,130]{0,1:T(8,128)}, f32[322,130]{0,1:T(8,128)S(1)}, u32[]{:S(2)}) copy-start(f32[322,130]{0,1:T(8,128)S(1)} %get-tuple-element.78) | copy-start | bytes 502324
  42.4 22.5 %copy-start.10 = (f32[322,130]{0,1:T(8,128)}, f32[322,130]{0,1:T(8,128)S(1)}, u32[]{:S(2)}) copy-start(f32[322,130]{0,1:T(8,128)S(1)} %get-tuple-element.79) | copy-start | bytes 502324
  42.5 8.5 %copy-start.17 = (f32[320,128]{0,1:T(8,128)S(1)}, f32[320,128]{0,1:T(8,128)}, u32[]{:S(2)}) copy-start(f32[320,128]{0,1:T(8,128)} %copy-done.16) | copy-start | bytes 491524
  42.5 8.5 %copy-start.23 = (s32[320,128]{0,1:T(8,128)S(1)}, s32[320,128]{0,1:T(8,128)}, u32[]{:S(2)}) copy-start(s32[320,128]{0,1:T(8,128)} %copy-done.22) | copy-start | bytes 491524
  42.5 8.5 %copy-start.26 = (f32[320,128]{0,1:T(8,128)S(1)}, f32[320,128]{0,1:T(8,128)}, u32[]{:S(2)}) copy-start(f32[320,128]{0,1:T(8,128)} %copy.48) | copy-start | bytes 491524
  52.5 14.1 %copy-start.20 = (f32[320,128]{0,1:T(8,128)}, f32[320,128]{0,1:T(8,128)S(1)}, u32[]{:S(2)}) copy-start(f32[320,128]{0,1:T(8,128)S(1)} %get-tuple-element.63) | copy-start | bytes 491524
  52.5 14.1 %copy-start.25 = (f32[320,128]{0,1:T(8,128)}, f32[320,128]{0,1:T(8,128)S(1)}, u32[]{:S(2)}) copy-start(f32[320,128]{0,1:T(8,128)S(1)} %get-tuple-element.64) | copy-start | bytes 491524
  52.5 10.4 %collective-permute-start.8 = (f32[320,1]{0,1:T(1,128)S(1)}, f32[320,1]{0,1:T(1,128)S(1)}, u32[]{:S(2)}, u32[]{:S(2)}) collective-permute-start(f32[320,1]{0,1:T(1,128)S(1)} %get-tuple-element.104), channel_id=1, source_target_pairs={{8,0},{16,8},{24,16},{32,24},{40,32},{48,40},{56,48},{64,56},{72,6... | collective-permute-start | bytes 3848 | tf_op jit(solution)/shard_map/ppermute | solution.py:51
  57.9 6.9 %collective-permute-start.9 = (f32[320,1]{0,1:T(1,128)S(1)}, f32[320,1]{0,1:T(1,128)S(1)}, u32[]{:S(2)}, u32[]{:S(2)}) collective-permute-start(f32[320,1]{0,1:T(1,128)S(1)} %get-tuple-element.103), channel_id=1, source_target_pairs={{0,8},{8,16},{16,24},{24,32},{32,40},{40,48},{48,56},{56,64},{64,7... | collective-permute-start | bytes 3848 | tf_op jit(solution)/shard_map/ppermute | solution.py:50
  58.0 4.9 %collective-permute-start.11 = (f32[1,128]{0,1:T(8,128)S(1)}, f32[1,128]{0,1:T(8,128)S(1)}, u32[]{:S(2)}, u32[]{:S(2)}) collective-permute-start(f32[1,128]{0,1:T(8,128)S(1)} %get-tuple-element.102), channel_id=1, source_target_pairs={{0,1},{1,2},{2,3},{3,4},{4,5},{5,6},{6,7},{7,0},{8,9},{9,10},{10,1... | collective-permute-start | bytes 1544 | tf_op jit(solution)/shard_map/ppermute | solution.py:50
  58.0 4.9 %collective-permute-start.10 = (f32[1,128]{0,1:T(8,128)S(1)}, f32[1,128]{0,1:T(8,128)S(1)}, u32[]{:S(2)}, u32[]{:S(2)}) collective-permute-start(f32[1,128]{0,1:T(8,128)S(1)} %get-tuple-element.101), channel_id=1, source_target_pairs={{1,0},{2,1},{3,2},{4,3},{5,4},{6,5},{7,6},{0,7},{9,8},{10,9},{11,1... | collective-permute-start | bytes 1544 | tf_op jit(solution)/shard_map/ppermute | solution.py:51
  101.2 7.1 %copy-start.15 = (f32[320,128]{0,1:T(8,128)}, f32[320,128]{0,1:T(8,128)S(1)}, u32[]{:S(2)}) copy-start(f32[320,128]{0,1:T(8,128)S(1)} %get-tuple-element.60) | copy-start | bytes 491524
  101.2 10.2 %copy-start.21 = (f32[320,128]{0,1:T(8,128)}, f32[320,128]{0,1:T(8,128)S(1)}, u32[]{:S(2)}) copy-start(f32[320,128]{0,1:T(8,128)S(1)} %get-tuple-element.61) | copy-start | bytes 491524
  101.2 7.1 %collective-permute-start.12 = (f32[320,1]{0,1:T(1,128)S(1)}, f32[320,1]{0,1:T(1,128)S(1)}, u32[]{:S(2)}, u32[]{:S(2)}) collective-permute-start(f32[320,1]{0,1:T(1,128)S(1)} %get-tuple-element.100), channel_id=1, source_target_pairs={{8,0},{16,8},{24,16},{32,24},{40,32},{48,40},{56,48},{64,56},{72,6... | collective-permute-start | bytes 3848 | tf_op jit(solution)/shard_map/ppermute | solution.py:51
  101.3 7.0 %collective-permute-start.13 = (f32[320,1]{0,1:T(1,128)S(1)}, f32[320,1]{0,1:T(1,128)S(1)}, u32[]{:S(2)}, u32[]{:S(2)}) collective-permute-start(f32[320,1]{0,1:T(1,128)S(1)} %get-tuple-element.99), channel_id=1, source_target_pairs={{0,8},{8,16},{16,24},{24,32},{32,40},{40,48},{48,56},{56,64},{64,7... | collective-permute-start | bytes 3848 | tf_op jit(solution)/shard_map/ppermute | solution.py:50
  103.4 4.9 %collective-permute-start.15 = (f32[1,128]{0,1:T(8,128)S(1)}, f32[1,128]{0,1:T(8,128)S(1)}, u32[]{:S(2)}, u32[]{:S(2)}) collective-permute-start(f32[1,128]{0,1:T(8,128)S(1)} %get-tuple-element.98), channel_id=1, source_target_pairs={{0,1},{1,2},{2,3},{3,4},{4,5},{5,6},{6,7},{7,0},{8,9},{9,10},{10,1... | collective-permute-start | bytes 1544 | tf_op jit(solution)/shard_map/ppermute | solution.py:50
  103.4 4.9 %collective-permute-start.14 = (f32[1,128]{0,1:T(8,128)S(1)}, f32[1,128]{0,1:T(8,128)S(1)}, u32[]{:S(2)}, u32[]{:S(2)}) collective-permute-start(f32[1,128]{0,1:T(8,128)S(1)} %get-tuple-element.97), channel_id=1, source_target_pairs={{1,0},{2,1},{3,2},{4,3},{5,4},{6,5},{7,6},{0,7},{9,8},{10,9},{11,1... | collective-permute-start | bytes 1544 | tf_op jit(solution)/shard_map/ppermute | solution.py:51
  148.8 9.0 %copy-start.2 = (f32[322,130]{0,1:T(8,128)S(1)}, f32[322,130]{0,1:T(8,128)}, u32[]{:S(2)}) copy-start(f32[322,130]{0,1:T(8,128)} %copy-done.1) | copy-start | bytes 502324
  148.9 9.0 %copy-start.5 = (f32[322,130]{0,1:T(8,128)S(1)}, f32[322,130]{0,1:T(8,128)}, u32[]{:S(2)}) copy-start(f32[322,130]{0,1:T(8,128)} %copy-done.4) | copy-start | bytes 502324
  148.9 9.0 %copy-start.8 = (f32[322,130]{0,1:T(8,128)S(1)}, f32[322,130]{0,1:T(8,128)}, u32[]{:S(2)}) copy-start(f32[322,130]{0,1:T(8,128)} %copy-done.7) | copy-start | bytes 502324
  148.9 9.0 %copy-start.11 = (f32[322,130]{0,1:T(8,128)S(1)}, f32[322,130]{0,1:T(8,128)}, u32[]{:S(2)}) copy-start(f32[322,130]{0,1:T(8,128)} %copy-done.10) | copy-start | bytes 502324
  150.1 9.5 %copy-start.18 = (f32[320,128]{0,1:T(8,128)}, f32[320,128]{0,1:T(8,128)S(1)}, u32[]{:S(2)}) copy-start(f32[320,128]{0,1:T(8,128)S(1)} %get-tuple-element.57) | copy-start | bytes 491524
  150.1 9.5 %copy-start.24 = (f32[320,128]{0,1:T(8,128)}, f32[320,128]{0,1:T(8,128)S(1)}, u32[]{:S(2)}) copy-start(f32[320,128]{0,1:T(8,128)S(1)} %get-tuple-element.58) | copy-start | bytes 491524
  150.3 7.0 %collective-permute-start.16 = (f32[320,1]{0,1:T(1,128)S(1)}, f32[320,1]{0,1:T(1,128)S(1)}, u32[]{:S(2)}, u32[]{:S(2)}) collective-permute-start(f32[320,1]{0,1:T(1,128)S(1)} %get-tuple-element.96), channel_id=1, source_target_pairs={{8,0},{16,8},{24,16},{32,24},{40,32},{48,40},{56,48},{64,56},{72,6... | collective-permute-start | bytes 3848 | tf_op jit(solution)/shard_map/ppermute | solution.py:51
  151.0 6.9 %collective-permute-start.17 = (f32[320,1]{0,1:T(1,128)S(1)}, f32[320,1]{0,1:T(1,128)S(1)}, u32[]{:S(2)}, u32[]{:S(2)}) collective-permute-start(f32[320,1]{0,1:T(1,128)S(1)} %get-tuple-element.95), channel_id=1, source_target_pairs={{0,8},{8,16},{16,24},{24,32},{32,40},{40,48},{48,56},{56,64},{64,7... | collective-permute-start | bytes 3848 | tf_op jit(solution)/shard_map/ppermute | solution.py:50
  152.3 4.9 %collective-permute-start.19 = (f32[1,128]{0,1:T(8,128)S(1)}, f32[1,128]{0,1:T(8,128)S(1)}, u32[]{:S(2)}, u32[]{:S(2)}) collective-permute-start(f32[1,128]{0,1:T(8,128)S(1)} %get-tuple-element.94), channel_id=1, source_target_pairs={{0,1},{1,2},{2,3},{3,4},{4,5},{5,6},{6,7},{7,0},{8,9},{9,10},{10,1... | collective-permute-start | bytes 1544 | tf_op jit(solution)/shard_map/ppermute | solution.py:50
  152.3 4.9 %collective-permute-start.18 = (f32[1,128]{0,1:T(8,128)S(1)}, f32[1,128]{0,1:T(8,128)S(1)}, u32[]{:S(2)}, u32[]{:S(2)}) collective-permute-start(f32[1,128]{0,1:T(8,128)S(1)} %get-tuple-element.93), channel_id=1, source_target_pairs={{1,0},{2,1},{3,2},{4,3},{5,4},{6,5},{7,6},{0,7},{9,8},{10,9},{11,1... | collective-permute-start | bytes 1544 | tf_op jit(solution)/shard_map/ppermute | solution.py:51
  195.7 11.2 %copy-start.3 = (f32[322,130]{0,1:T(8,128)S(1)}, f32[322,130]{0,1:T(8,128)}, u32[]{:S(2)}) copy-start(f32[322,130]{0,1:T(8,128)} %copy-done.1) | copy-start | bytes 502324
  195.7 12.0 %copy-start.6 = (f32[322,130]{0,1:T(8,128)S(1)}, f32[322,130]{0,1:T(8,128)}, u32[]{:S(2)}) copy-start(f32[322,130]{0,1:T(8,128)} %copy-done.4) | copy-start | bytes 502324
  195.7 12.0 %copy-start.9 = (f32[322,130]{0,1:T(8,128)S(1)}, f32[322,130]{0,1:T(8,128)}, u32[]{:S(2)}) copy-start(f32[322,130]{0,1:T(8,128)} %copy-done.7) | copy-start | bytes 502324
  195.7 12.0 %copy-start.12 = (f32[322,130]{0,1:T(8,128)S(1)}, f32[322,130]{0,1:T(8,128)}, u32[]{:S(2)}) copy-start(f32[322,130]{0,1:T(8,128)} %copy-done.10) | copy-start | bytes 502324
  197.1 11.6 %copy-start.19 = (f32[320,128]{0,1:T(8,128)}, f32[320,128]{0,1:T(8,128)S(1)}, u32[]{:S(2)}) copy-start(f32[320,128]{0,1:T(8,128)S(1)} %get-tuple-element.54) | copy-start | bytes 491524
  197.2 10.5 %collective-permute-start.23 = (f32[1,128]{0,1:T(8,128)S(1)}, f32[1,128]{0,1:T(8,128)S(1)}, u32[]{:S(2)}, u32[]{:S(2)}) collective-permute-start(f32[1,128]{0,1:T(8,128)S(1)} %get-tuple-element.90), channel_id=1, source_target_pairs={{0,1},{1,2},{2,3},{3,4},{4,5},{5,6},{6,7},{7,0},{8,9},{9,10},{10,1... | collective-permute-start | bytes 1544 | tf_op jit(solution)/shard_map/ppermute | solution.py:50
  197.4 10.3 %collective-permute-start.20 = (f32[320,1]{0,1:T(1,128)S(1)}, f32[320,1]{0,1:T(1,128)S(1)}, u32[]{:S(2)}, u32[]{:S(2)}) collective-permute-start(f32[320,1]{0,1:T(1,128)S(1)} %get-tuple-element.92), channel_id=1, source_target_pairs={{8,0},{16,8},{24,16},{32,24},{40,32},{48,40},{56,48},{64,56},{72,6... | collective-permute-start | bytes 3848 | tf_op jit(solution)/shard_map/ppermute | solution.py:51
  197.5 10.1 %collective-permute-start.21 = (f32[320,1]{0,1:T(1,128)S(1)}, f32[320,1]{0,1:T(1,128)S(1)}, u32[]{:S(2)}, u32[]{:S(2)}) collective-permute-start(f32[320,1]{0,1:T(1,128)S(1)} %get-tuple-element.91), channel_id=1, source_target_pairs={{0,8},{8,16},{16,24},{24,32},{32,40},{40,48},{48,56},{56,64},{64,7... | collective-permute-start | bytes 3848 | tf_op jit(solution)/shard_map/ppermute | solution.py:50
  199.4 8.3 %collective-permute-start.22 = (f32[1,128]{0,1:T(8,128)S(1)}, f32[1,128]{0,1:T(8,128)S(1)}, u32[]{:S(2)}, u32[]{:S(2)}) collective-permute-start(f32[1,128]{0,1:T(8,128)S(1)} %get-tuple-element.89), channel_id=1, source_target_pairs={{1,0},{2,1},{3,2},{4,3},{5,4},{6,5},{7,6},{0,7},{9,8},{10,9},{11,1... | collective-permute-start | bytes 1544 | tf_op jit(solution)/shard_map/ppermute | solution.py:51
  248.3 10.5 %collective-permute-start.26 = (f32[1,128]{0,1:T(8,128)}, f32[1,128]{0,1:T(8,128)}, u32[]{:S(2)}, u32[]{:S(2)}) collective-permute-start(f32[1,128]{0,1:T(8,128)} %slice.452), channel_id=1, source_target_pairs={{1,0},{2,1},{3,2},{4,3},{5,4},{6,5},{7,6},{0,7},{9,8},{10,9},{11,1... | collective-permute-start | bytes 1544 | tf_op jit(solution)/shard_map/ppermute | solution.py:51
  249.3 9.5 %collective-permute-start.24 = (f32[320,1]{0,1:T(1,128)}, f32[320,1]{0,1:T(1,128)S(1)}, u32[]{:S(2)}, u32[]{:S(2)}) collective-permute-start(f32[320,1]{0,1:T(1,128)} %get-tuple-element.87), channel_id=1, source_target_pairs={{8,0},{16,8},{24,16},{32,24},{40,32},{48,40},{56,48},{64,56},{72,6... | collective-permute-start | bytes 3848 | tf_op jit(solution)/shard_map/ppermute | solution.py:51
  249.3 9.5 %collective-permute-start.25 = (f32[320,1]{0,1:T(1,128)}, f32[320,1]{0,1:T(1,128)S(1)}, u32[]{:S(2)}, u32[]{:S(2)}) collective-permute-start(f32[320,1]{0,1:T(1,128)} %get-tuple-element.86), channel_id=1, source_target_pairs={{0,8},{8,16},{16,24},{24,32},{32,40},{40,48},{48,56},{56,64},{64,7... | collective-permute-start | bytes 3848 | tf_op jit(solution)/shard_map/ppermute | solution.py:50
  255.7 4.1 %copy-start.14 = (f32[4,322,130]{1,2,0:T(8,128)S(1)}, f32[4,322,130]{1,2,0:T(8,128)}, u32[]{:S(2)}) copy-start(f32[4,322,130]{1,2,0:T(8,128)} %get-tuple-element.66) | copy-start | bytes 2009284
where the time goes:
time: 267 us; the launch traced here: 266 us
  blocking collectives  131 us (49%)
  starting transfers between devices  43.2 us (16%)
  other arithmetic  38.9 us (15%)
  local copies, waits for them, and re-layouts  30.2 us (11%)
  between operations  14.8 us (6%)
  waiting for transfers between devices  8.19 us (3%)
    psum x16, blocking collectives, one_axis_at_a_time(): x = lax.psum(x, axis)  131 us
    ppermute x12, starting transfers between devices, padded_3(): lax.ppermute(first, axis, [(b, a) for a, b in up])  26.7 us
    unnamed x69, local copies, waits for them, and re-layouts  14.5 us
    ppermute x2, starting transfers between devices, padded_2(): lax.ppermute(head, axis, [((i + 1) % count, i) for i in range(count)])  9.01 us
    reduce_sum x1, other arithmetic, on_device(): east_flow = wet_cycle * jnp.sum(thick * u_star, 0)  8.32 us
    ppermute x11, waiting for transfers between devices, padded_3(): lax.ppermute(last, axis, up)  7.52 us
    reduce_sum x4, other arithmetic, pair_totals(): jnp.sum(precond * image)  7.51 us
    ppermute x11, starting transfers between devices, padded_3(): lax.ppermute(last, axis, up)  7.45 us
  transfers between devices with their start and end apart: 27, of which 6 were waited for; matrix products, arithmetic and copies ran while one was open for 14% of the time, Pallas kernels for 0%

commit v1 on v0

--- a/solution.py
+++ b/solution.py
@@ -17,9 +17,15 @@
 gravity = 1.0
 
 
+def gather_and_add(value, axis):
+    pieces = lax.all_gather(value, axis, axis=0, tiled=False)
+    total = pieces.sum(axis=0)
+    return total
+
+
 def one_axis_at_a_time(x, axes):
     for axis in axes:
-        x = lax.psum(x, axis)
+        x = gather_and_add(x, axis)
     return x
 
 

time: 267 us -> 353 us (1.32)
  local copies, waits for them, and re-layouts: 30.2 us -> 98.9 us
  other arithmetic: 38.9 us -> 62.4 us
  blocking collectives: 131 us -> 122 us
    psum x16 -> x0, blocking collectives: 131 us -> none  [one_axis_at_a_time(): x = lax.psum(x, axis)]
    unnamed x0 -> x16, blocking collectives: none -> 122 us
    unnamed x69 -> x159, local copies, waits for them, and re-layouts: 14.5 us -> 81.7 us
    reduce_sum x0 -> x32, other arithmetic: none -> 20.2 us  [gather_and_add(): total = pieces.sum(axis=0)]
  transfers between devices with their start and end apart: 27 -> 27, of which waited for: 6 -> 9; matrix products, arithmetic and copies ran while one was open for 14% -> 10% of each run, Pallas kernels for 0% -> 0%
where the time goes in v1:
time: 353 us; the launch traced here: 351 us
  blocking collectives  122 us (35%)
  local copies, waits for them, and re-layouts  98.9 us (28%)
  other arithmetic  62.4 us (18%)
  starting transfers between devices  43.2 us (12%)
  between operations  15.2 us (4%)
  waiting for transfers between devices  9.18 us (3%)
    unnamed x16, blocking collectives  122 us
    unnamed x159, local copies, waits for them, and re-layouts  81.7 us
    ppermute x12, starting transfers between devices, padded_3(): lax.ppermute(first, axis, [(b, a) for a, b in up])  27 us
    reduce_sum x32, other arithmetic, gather_and_add(): total = pieces.sum(axis=0)  20.2 us
    reduce_sum x4, other arithmetic, pair_totals(): jnp.sum(precond * image)  10.4 us
    ppermute x2, starting transfers between devices, padded_2(): lax.ppermute(head, axis, [((i + 1) % count, i) for i in range(count)])  8.99 us
    reduce_sum x1, other arithmetic, on_device(): east_flow = wet_cycle * jnp.sum(thick * u_star, 0)  8.29 us
    ppermute x11, starting transfers between devices, padded_3(): lax.ppermute(last, axis, up)  7.22 us
  transfers between devices with their start and end apart: 27, of which 9 were waited for; matrix products, arithmetic and copies ran while one was open for 10% of the time, Pallas kernels for 0%

profile of v1, /device:TPU:0, one launch (start us, length us, event | category | flops | bytes accessed | tf_op | source)
XLA Modules:
  0.0 350.5 jit_solution(1451367002350614986)
XLA Ops:
  9.5 6.7 %collective-permute-start.1 = (f32[13,320,2]{1,2,0:T(2,128)S(1)}, f32[13,320,2]{1,2,0:T(2,128)S(1)}, u32[]{:S(2)}, u32[]{:S(2)}) collective-permute-start(f32[13,320,2]{1,2,0:T(2,128)S(1)} %get-tuple-element.73), channel_id=1, source_target_pairs={{8,0},{16,8},{24,16},{32,24},{40,32},{48,40},{56,48},{64,56},{72,6... | collective-permute-start | bytes 99848 | tf_op jit(solution)/shard_map/ppermute | solution.py:41
  16.8 5.3 %collective-permute-start.4 = (f32[320,1]{0,1:T(1,128)}, f32[320,1]{0,1:T(1,128)}, u32[]{:S(2)}, u32[]{:S(2)}) collective-permute-start(f32[320,1]{0,1:T(1,128)} %get-tuple-element.108), channel_id=1, source_target_pairs={{8,0},{16,8},{24,16},{32,24},{40,32},{48,40},{56,48},{64,56},{72,6... | collective-permute-start | bytes 3848 | tf_op jit(solution)/shard_map/ppermute | solution.py:57
  24.8 2.3 copy.42
  27.1 2.3 collective-permute-start.3
  31.0 1.7 copy.48
  32.7 3.0 collective-permute-start.6
  36.8 2.0 copy.43
  38.8 2.3 pad_maximum_fusion
  42.4 8.3 %multiply_reduce_fusion.1 = (f32[322,130]{0,1:T(8,128)S(1)}, f32[322,130]{0,1:T(8,128)S(1)}, f32[4,322,130]{1,2,0:T(8,128)}, f32[4,322,130]{1,2,0:T(8,128)}) fusion(f32[4]{0:T(128)S(1)} %copy-done.24, f32[13,324,132]{1,2,0:T(8,128)S(1)} %pad_maximum_fusion, f32[322]{0:T(512)S(1)} %fusion.91, f32[13,320,2]{1,2,0:T(2,128)S(1)} %collective-permute-done.1, ...), kind=kLoop, calls=%fused_computation.40 | loop fusion | flops 10632440 | bytes 9592600 | tf_op jit(solution)/shard_map/reduce_sum | solution.py:187
  50.9 2.2 fusion.102
  53.1 5.4 %collective-permute-start.8 = (f32[320,1]{0,1:T(1,128)S(1)}, f32[320,1]{0,1:T(1,128)}, u32[]{:S(2)}, u32[]{:S(2)}) collective-permute-start(f32[320,1]{0,1:T(1,128)S(1)} %get-tuple-element.104), channel_id=1, source_target_pairs={{8,0},{16,8},{24,16},{32,24},{40,32},{48,40},{56,48},{64,56},{72,6... | collective-permute-start | bytes 3848 | tf_op jit(solution)/shard_map/ppermute | solution.py:57
  59.2 3.0 collective-permute-start.10
  65.5 3.3 multiply_reduce_fusion.7
  73.3 7.8 %all-reduce.60 = (f32[4]{0:T(128)S(1)}, f32[4]{0:T(128)S(1)}) all-reduce(f32[4]{0:T(128)} %copy-done.25, f32[4]{0:T(128)} %copy-done.26), channel_id=1, replica_groups=mesh['gx_0'=4,'gx_1'=4,'gy_0'=4,'gy_1'=2] {'gx_0'}, use_global_device_ids=true, to_apply=%add.17 | all-reduce | flops 8 | bytes 64
  87.0 12.7 %all-reduce.56 = (f32[4]{0:T(128)S(1)}, f32[4]{0:T(128)S(1)}) all-reduce(f32[4]{0:T(128)} %copy-done.27, f32[4]{0:T(128)} %copy-done.28), channel_id=1, replica_groups=mesh['gx_0'=4,'gx_1'=4,'gy_0'=4,'gy_1'=2] {'gx_1'}, use_global_device_ids=true, to_apply=%add.18 | all-reduce | flops 8 | bytes 64
  101.0 1.4 dynamic-update-slice.2
  105.7 7.8 %all-reduce.52 = (f32[4]{0:T(128)S(1)}, f32[4]{0:T(128)S(1)}) all-reduce(f32[4]{0:T(128)} %copy-done.29, f32[4]{0:T(128)} %copy-done.30), channel_id=1, replica_groups=mesh['gx_0'=4,'gx_1'=4,'gy_0'=4,'gy_1'=2] {'gy_0'}, use_global_device_ids=true, to_apply=%add.19 | all-reduce | flops 8 | bytes 64
  116.7 2.6 dynamic-update-slice.7
  119.3 2.6 all-reduce.64
  125.6 2.0 collective-permute-start.13
  127.7 3.0 collective-permute-start.14
  130.6 1.9 collective-permute-done.15
  132.6 3.0 multiply_reduce_fusion.5
  137.5 2.5 dynamic-update-slice.12
  140.0 7.8 %all-reduce.59 = (f32[4]{0:T(128)S(1)}, f32[4]{0:T(128)S(1)}) all-reduce(f32[4]{0:T(128)} %copy-done.32, f32[4]{0:T(128)} %dynamic-update-slice.12), channel_id=1, replica_groups=mesh['gx_0'=4,'gx_1'=4,'gy_0'=4,'gy_1'=2] {'gx_0'}, use_global_device_ids=true, to_apply=%add.25 | all-reduce | flops 8 | bytes 64
  151.1 2.5 dynamic-update-slice.13
  153.6 11.8 %all-reduce.55 = (f32[4]{0:T(128)S(1)}, f32[4]{0:T(128)S(1)}) all-reduce(f32[4]{0:T(128)} %copy-done.33, f32[4]{0:T(128)} %dynamic-update-slice.13), channel_id=1, replica_groups=mesh['gx_0'=4,'gx_1'=4,'gy_0'=4,'gy_1'=2] {'gx_1'}, use_global_device_ids=true, to_apply=%add.26 | all-reduce | flops 8 | bytes 64
  166.1 1.5 dynamic-update-slice.10
  168.7 2.6 dynamic-update-slice.14
  171.3 8.6 %all-reduce.51 = (f32[4]{0:T(128)S(1)}, f32[4]{0:T(128)S(1)}) all-reduce(f32[4]{0:T(128)} %copy-done.34, f32[4]{0:T(128)} %dynamic-update-slice.14), channel_id=1, replica_groups=mesh['gx_0'=4,'gx_1'=4,'gy_0'=4,'gy_1'=2] {'gy_0'}, use_global_device_ids=true, to_apply=%add.27 | all-reduce | flops 8 | bytes 64
  180.6 1.4 dynamic-update-slice.11
  183.2 2.5 dynamic-update-slice.15
  185.7 2.6 all-reduce.63
  197.8 3.0 collective-permute-start.18
  203.3 1.7 multiply_reduce_fusion.3
  206.9 2.6 dynamic-update-slice.20
  209.5 7.8 %all-reduce.58 = (f32[4]{0:T(128)S(1)}, f32[4]{0:T(128)S(1)}) all-reduce(f32[4]{0:T(128)} %copy-done.36, f32[4]{0:T(128)} %dynamic-update-slice.20), channel_id=1, replica_groups=mesh['gx_0'=4,'gx_1'=4,'gy_0'=4,'gy_1'=2] {'gx_0'}, use_global_device_ids=true, to_apply=%add.33 | all-reduce | flops 8 | bytes 64
  220.4 2.4 dynamic-update-slice.21
  222.8 11.8 %all-reduce.54 = (f32[4]{0:T(128)S(1)}, f32[4]{0:T(128)S(1)}) all-reduce(f32[4]{0:T(128)} %copy-done.37, f32[4]{0:T(128)} %dynamic-update-slice.21), channel_id=1, replica_groups=mesh['gx_0'=4,'gx_1'=4,'gy_0'=4,'gy_1'=2] {'gx_1'}, use_global_device_ids=true, to_apply=%add.34 | all-reduce | flops 8 | bytes 64
  235.2 1.4 dynamic-update-slice.18
  237.7 2.4 dynamic-update-slice.22
  240.2 7.8 %all-reduce.50 = (f32[4]{0:T(128)S(1)}, f32[4]{0:T(128)S(1)}) all-reduce(f32[4]{0:T(128)} %copy-done.38, f32[4]{0:T(128)} %dynamic-update-slice.22), channel_id=1, replica_groups=mesh['gx_0'=4,'gx_1'=4,'gy_0'=4,'gy_1'=2] {'gy_0'}, use_global_device_ids=true, to_apply=%add.35 | all-reduce | flops 8 | bytes 64
  251.2 2.4 dynamic-update-slice.23
  253.5 2.6 all-reduce.62
  263.3 1.9 collective-permute-start.21
  265.1 2.2 collective-permute-start.22
  267.8 1.4 collective-permute-done.22
  270.2 2.3 fusion.35
  275.2 1.7 slice.428
  276.9 7.7 %all-reduce.57 = (f32[4]{0:T(128)S(1)}, f32[4]{0:T(128)S(1)}) all-reduce(f32[4]{0:T(128)S(1)} %dynamic-update-slice.24, f32[4]{0:T(128)S(1)} %dynamic-update-slice.28), channel_id=1, replica_groups=mesh['gx_0'=4,'gx_1'=4,'gy_0'=4,'gy_1'=2] {'gx_0'}, use_global_device_ids=true, to_apply=%add.41 | all-reduce | flops 8 | bytes 64
  288.6 1.7 slice.427
  290.3 11.0 %all-reduce.53 = (f32[4]{0:T(128)S(1)}, f32[4]{0:T(128)S(1)}) all-reduce(f32[4]{0:T(128)S(1)} %dynamic-update-slice.25, f32[4]{0:T(128)S(1)} %dynamic-update-slice.29), channel_id=1, replica_groups=mesh['gx_0'=4,'gx_1'=4,'gy_0'=4,'gy_1'=2] {'gx_1'}, use_global_device_ids=true, to_apply=%add.42 | all-reduce | flops 8 | bytes 64
  301.9 1.4 dynamic-update-slice.26
  304.0 1.4 dynamic-update-slice.30
  305.4 1.7 slice.426
  307.1 8.5 %all-reduce.49 = (f32[4]{0:T(128)S(1)}, f32[4]{0:T(128)S(1)}) all-reduce(f32[4]{0:T(128)S(1)} %dynamic-update-slice.26, f32[4]{0:T(128)S(1)} %dynamic-update-slice.30), channel_id=1, replica_groups=mesh['gx_0'=4,'gx_1'=4,'gy_0'=4,'gy_1'=2] {'gy_0'}, use_global_device_ids=true, to_apply=%add.43 | all-reduce | flops 8 | bytes 64
  319.8 1.7 slice.425
  321.5 2.7 all-reduce.61
  333.1 1.8 collective-permute-start.25
  334.9 4.4 %multiply_add_fusion = f32[4,320,128]{1,2,0:T(8,128)} fusion(f32[4,320,128]{1,2,0:T(8,128)S(1)} %copy.40, f32[4,320,128]{1,2,0:T(8,128)S(1)} %copy.39, f32[4,320,128]{1,2,0:T(8,128)S(1)} %copy.38, f32[13,320,2]{1,2,0:T(2,128)S(1)} %collective-permute-done.1, f32[1,320,128]{1,2,0:T(8,128)} %copy-done.9, f32[13,320,2]{1,2,0:T(2,128)S(1)} %collective-permute-done, ...), kind=kLoop, calls=%fused_computation.67 | loop fusion | flops 7536640 | bytes 4191296 | tf_op jit(solution)/shard_map/add | solution.py:217
  339.3 2.4 copy.63
  343.5 2.6 fusion.25
  346.1 2.2 copy.61
  348.3 2.2 copy.62
  (248 shorter events, 89.8 us)
Async XLA Ops:
  0.6 6.5 %copy-start.23 = (f32[4,320,128]{2,1,0:T(8,128)S(1)}, f32[4,320,128]{2,1,0:T(8,128)}, u32[]{:S(2)}) copy-start(f32[4,320,128]{2,1,0:T(8,128)} %param.10) | copy-start | bytes 1966084
  2.8 6.7 %copy-start.19 = (s32[320,128]{0,1:T(8,128)}, s32[320,128]{0,1:T(8,128)S(1)}, u32[]{:S(2)}) copy-start(s32[320,128]{0,1:T(8,128)S(1)} %copy.36) | copy-start | bytes 491524
  9.5 13.4 %copy-start.13 = (f32[320,128]{0,1:T(8,128)}, f32[320,128]{0,1:T(8,128)S(1)}, u32[]{:S(2)}) copy-start(f32[320,128]{0,1:T(8,128)S(1)} %get-tuple-element.82) | copy-start | bytes 491524
  9.5 32.8 %copy-start.9 = (f32[1,320,128]{1,2,0:T(8,128)}, f32[1,320,128]{1,2,0:T(8,128)S(1)}, u32[]{:S(2)}) copy-start(f32[1,320,128]{1,2,0:T(8,128)S(1)} %get-tuple-element.83) | copy-start | bytes 491524
  9.5 13.3 %collective-permute-start.1 = (f32[13,320,2]{1,2,0:T(2,128)S(1)}, f32[13,320,2]{1,2,0:T(2,128)S(1)}, u32[]{:S(2)}, u32[]{:S(2)}) collective-permute-start(f32[13,320,2]{1,2,0:T(2,128)S(1)} %get-tuple-element.73), channel_id=1, source_target_pairs={{8,0},{16,8},{24,16},{32,24},{40,32},{48,40},{56,48},{64,56},{72,6... | collective-permute-start | bytes 99848 | tf_op jit(solution)/shard_map/ppermute | solution.py:41
  16.2 7.3 %collective-permute-start = (f32[13,320,2]{1,2,0:T(2,128)S(1)}, f32[13,320,2]{1,2,0:T(2,128)S(1)}, u32[]{:S(2)}, u32[]{:S(2)}) collective-permute-start(f32[13,320,2]{1,2,0:T(2,128)S(1)} %get-tuple-element.72), channel_id=1, source_target_pairs={{0,8},{8,16},{16,24},{24,32},{32,40},{40,48},{48,56},{56,64},{64,7... | collective-permute-start | bytes 99848 | tf_op jit(solution)/shard_map/ppermute | solution.py:39
  16.8 34.0 %collective-permute-start.4 = (f32[320,1]{0,1:T(1,128)}, f32[320,1]{0,1:T(1,128)}, u32[]{:S(2)}, u32[]{:S(2)}) collective-permute-start(f32[320,1]{0,1:T(1,128)} %get-tuple-element.108), channel_id=1, source_target_pairs={{8,0},{16,8},{24,16},{32,24},{40,32},{48,40},{56,48},{64,56},{72,6... | collective-permute-start | bytes 3848 | tf_op jit(solution)/shard_map/ppermute | solution.py:57
  22.1 28.7 %collective-permute-start.5 = (f32[320,1]{0,1:T(1,128)}, f32[320,1]{0,1:T(1,128)}, u32[]{:S(2)}, u32[]{:S(2)}) collective-permute-start(f32[320,1]{0,1:T(1,128)} %get-tuple-element.107), channel_id=1, source_target_pairs={{0,8},{8,16},{16,24},{24,32},{32,40},{40,48},{48,56},{56,64},{64,7... | collective-permute-start | bytes 3848 | tf_op jit(solution)/shard_map/ppermute | solution.py:56
  22.8 28.0 %collective-permute-start.7 = (f32[1,128]{0,1:T(8,128)}, f32[1,128]{0,1:T(8,128)}, u32[]{:S(2)}, u32[]{:S(2)}) collective-permute-start(f32[1,128]{0,1:T(8,128)} %get-tuple-element.106), channel_id=1, source_target_pairs={{0,1},{1,2},{2,3},{3,4},{4,5},{5,6},{6,7},{7,0},{8,9},{9,10},{10,1... | collective-permute-start | bytes 1544 | tf_op jit(solution)/shard_map/ppermute | solution.py:56
  27.1 5.7 %collective-permute-start.3 = (f32[13,2,132]{2,1,0:T(2,128)}, f32[13,2,132]{2,1,0:T(2,128)}, u32[]{:S(2)}, u32[]{:S(2)}) collective-permute-start(f32[13,2,132]{2,1,0:T(2,128)} %copy.42), channel_id=1, source_target_pairs={{1,0},{2,1},{3,2},{4,3},{5,4},{6,5},{7,6},{0,7},{9,8},{10,9},{11,1... | collective-permute-start | bytes 41192 | tf_op jit(solution)/shard_map/ppermute | solution.py:41
  30.5 6.3 %collective-permute-start.2 = (f32[13,2,132]{2,1,0:T(2,128)}, f32[13,2,132]{2,1,0:T(2,128)}, u32[]{:S(2)}, u32[]{:S(2)}) collective-permute-start(f32[13,2,132]{2,1,0:T(2,128)} %copy.41), channel_id=1, source_target_pairs={{0,1},{1,2},{2,3},{3,4},{4,5},{5,6},{6,7},{7,0},{8,9},{9,10},{10,1... | collective-permute-start | bytes 41192 | tf_op jit(solution)/shard_map/ppermute | solution.py:39
  32.7 18.1 %collective-permute-start.6 = (f32[1,128]{0,1:T(8,128)}, f32[1,128]{0,1:T(8,128)}, u32[]{:S(2)}, u32[]{:S(2)}) collective-permute-start(f32[1,128]{0,1:T(8,128)} %get-tuple-element.105), channel_id=1, source_target_pairs={{1,0},{2,1},{3,2},{4,3},{5,4},{6,5},{7,6},{0,7},{9,8},{10,9},{11,1... | collective-permute-start | bytes 1544 | tf_op jit(solution)/shard_map/ppermute | solution.py:57
  41.2 1.2 copy-start
  41.2 1.2 copy-start.24
  42.2 8.6 %copy-start.1 = (f32[322,130]{0,1:T(8,128)}, f32[322,130]{0,1:T(8,128)S(1)}, u32[]{:S(2)}) copy-start(f32[322,130]{0,1:T(8,128)S(1)} %get-tuple-element.76) | copy-start | bytes 502324
  42.3 8.6 %copy-start.3 = (f32[322,130]{0,1:T(8,128)}, f32[322,130]{0,1:T(8,128)S(1)}, u32[]{:S(2)}) copy-start(f32[322,130]{0,1:T(8,128)S(1)} %get-tuple-element.79) | copy-start | bytes 502324
  42.3 8.6 %copy-start.5 = (f32[322,130]{0,1:T(8,128)}, f32[322,130]{0,1:T(8,128)S(1)}, u32[]{:S(2)}) copy-start(f32[322,130]{0,1:T(8,128)S(1)} %get-tuple-element.78) | copy-start | bytes 502324
  42.3 8.6 %copy-start.7 = (f32[322,130]{0,1:T(8,128)}, f32[322,130]{0,1:T(8,128)S(1)}, u32[]{:S(2)}) copy-start(f32[322,130]{0,1:T(8,128)S(1)} %get-tuple-element.77) | copy-start | bytes 502324
  42.4 8.5 %copy-start.14 = (f32[320,128]{0,1:T(8,128)S(1)}, f32[320,128]{0,1:T(8,128)}, u32[]{:S(2)}) copy-start(f32[320,128]{0,1:T(8,128)} %copy-done.13) | copy-start | bytes 491524
  42.4 8.5 %copy-start.20 = (s32[320,128]{0,1:T(8,128)S(1)}, s32[320,128]{0,1:T(8,128)}, u32[]{:S(2)}) copy-start(s32[320,128]{0,1:T(8,128)} %copy-done.19) | copy-start | bytes 491524
  42.4 8.5 %copy-start.22 = (f32[320,128]{0,1:T(8,128)S(1)}, f32[320,128]{0,1:T(8,128)}, u32[]{:S(2)}) copy-start(f32[320,128]{0,1:T(8,128)} %copy.48) | copy-start | bytes 491524
  53.1 5.4 %copy-start.17 = (f32[320,128]{0,1:T(8,128)}, f32[320,128]{0,1:T(8,128)S(1)}, u32[]{:S(2)}) copy-start(f32[320,128]{0,1:T(8,128)S(1)} %get-tuple-element.63) | copy-start | bytes 491524
  53.1 11.3 %collective-permute-start.8 = (f32[320,1]{0,1:T(1,128)S(1)}, f32[320,1]{0,1:T(1,128)}, u32[]{:S(2)}, u32[]{:S(2)}) collective-permute-start(f32[320,1]{0,1:T(1,128)S(1)} %get-tuple-element.104), channel_id=1, source_target_pairs={{8,0},{16,8},{24,16},{32,24},{40,32},{48,40},{56,48},{64,56},{72,6... | collective-permute-start | bytes 3848 | tf_op jit(solution)/shard_map/ppermute | solution.py:57
  58.5 7.0 %collective-permute-start.9 = (f32[320,1]{0,1:T(1,128)S(1)}, f32[320,1]{0,1:T(1,128)}, u32[]{:S(2)}, u32[]{:S(2)}) collective-permute-start(f32[320,1]{0,1:T(1,128)S(1)} %get-tuple-element.103), channel_id=1, source_target_pairs={{0,8},{8,16},{16,24},{24,32},{32,40},{40,48},{48,56},{56,64},{64,7... | collective-permute-start | bytes 3848 | tf_op jit(solution)/shard_map/ppermute | solution.py:56
  59.2 5.2 %collective-permute-start.11 = (f32[1,128]{0,1:T(8,128)}, f32[1,128]{0,1:T(8,128)}, u32[]{:S(2)}, u32[]{:S(2)}) collective-permute-start(f32[1,128]{0,1:T(8,128)} %get-tuple-element.102), channel_id=1, source_target_pairs={{0,1},{1,2},{2,3},{3,4},{4,5},{5,6},{6,7},{7,0},{8,9},{9,10},{10,1... | collective-permute-start | bytes 1544 | tf_op jit(solution)/shard_map/ppermute | solution.py:56
  59.2 5.2 %collective-permute-start.10 = (f32[1,128]{0,1:T(8,128)}, f32[1,128]{0,1:T(8,128)}, u32[]{:S(2)}, u32[]{:S(2)}) collective-permute-start(f32[1,128]{0,1:T(8,128)} %get-tuple-element.101), channel_id=1, source_target_pairs={{1,0},{2,1},{3,2},{4,3},{5,4},{6,5},{7,6},{0,7},{9,8},{10,9},{11,1... | collective-permute-start | bytes 1544 | tf_op jit(solution)/shard_map/ppermute | solution.py:57
  70.1 1.4 copy-start.25
  83.7 1.4 copy-start.27
  102.4 1.4 copy-start.29
  103.8 0.6 copy-start.30
  116.1 0.6 copy-start.31
  125.4 7.1 %copy-start.12 = (f32[320,128]{0,1:T(8,128)}, f32[320,128]{0,1:T(8,128)S(1)}, u32[]{:S(2)}) copy-start(f32[320,128]{0,1:T(8,128)S(1)} %get-tuple-element.60) | copy-start | bytes 491524
  125.4 10.1 %copy-start.18 = (f32[320,128]{0,1:T(8,128)}, f32[320,128]{0,1:T(8,128)S(1)}, u32[]{:S(2)}) copy-start(f32[320,128]{0,1:T(8,128)S(1)} %get-tuple-element.61) | copy-start | bytes 491524
  125.5 7.1 %collective-permute-start.12 = (f32[320,1]{0,1:T(1,128)S(1)}, f32[320,1]{0,1:T(1,128)S(1)}, u32[]{:S(2)}, u32[]{:S(2)}) collective-permute-start(f32[320,1]{0,1:T(1,128)S(1)} %get-tuple-element.100), channel_id=1, source_target_pairs={{8,0},{16,8},{24,16},{32,24},{40,32},{48,40},{56,48},{64,56},{72,6... | collective-permute-start | bytes 3848 | tf_op jit(solution)/shard_map/ppermute | solution.py:57
  125.6 7.0 %collective-permute-start.13 = (f32[320,1]{0,1:T(1,128)S(1)}, f32[320,1]{0,1:T(1,128)S(1)}, u32[]{:S(2)}, u32[]{:S(2)}) collective-permute-start(f32[320,1]{0,1:T(1,128)S(1)} %get-tuple-element.99), channel_id=1, source_target_pairs={{0,8},{8,16},{16,24},{24,32},{32,40},{40,48},{48,56},{56,64},{64,7... | collective-permute-start | bytes 3848 | tf_op jit(solution)/shard_map/ppermute | solution.py:56
  127.6 4.9 %collective-permute-start.15 = (f32[1,128]{0,1:T(8,128)S(1)}, f32[1,128]{0,1:T(8,128)S(1)}, u32[]{:S(2)}, u32[]{:S(2)}) collective-permute-start(f32[1,128]{0,1:T(8,128)S(1)} %get-tuple-element.98), channel_id=1, source_target_pairs={{0,1},{1,2},{2,3},{3,4},{4,5},{5,6},{6,7},{7,0},{8,9},{9,10},{10,1... | collective-permute-start | bytes 1544 | tf_op jit(solution)/shard_map/ppermute | solution.py:56
  127.7 4.9 %collective-permute-start.14 = (f32[1,128]{0,1:T(8,128)S(1)}, f32[1,128]{0,1:T(8,128)S(1)}, u32[]{:S(2)}, u32[]{:S(2)}) collective-permute-start(f32[1,128]{0,1:T(8,128)S(1)} %get-tuple-element.97), channel_id=1, source_target_pairs={{1,0},{2,1},{3,2},{4,3},{5,4},{6,5},{7,6},{0,7},{9,8},{10,9},{11,1... | collective-permute-start | bytes 1544 | tf_op jit(solution)/shard_map/ppermute | solution.py:57
  150.0 1.2 copy-start.33
  167.6 1.2 copy-start.34
  182.1 1.2 copy-start.35
  194.3 9.0 %copy-start.2 = (f32[322,130]{0,1:T(8,128)S(1)}, f32[322,130]{0,1:T(8,128)}, u32[]{:S(2)}) copy-start(f32[322,130]{0,1:T(8,128)} %copy-done.1) | copy-start | bytes 502324
  194.3 9.0 %copy-start.4 = (f32[322,130]{0,1:T(8,128)S(1)}, f32[322,130]{0,1:T(8,128)}, u32[]{:S(2)}) copy-start(f32[322,130]{0,1:T(8,128)} %copy-done.3) | copy-start | bytes 502324
  194.3 9.0 %copy-start.6 = (f32[322,130]{0,1:T(8,128)S(1)}, f32[322,130]{0,1:T(8,128)}, u32[]{:S(2)}) copy-start(f32[322,130]{0,1:T(8,128)} %copy-done.5) | copy-start | bytes 502324
  194.3 9.0 %copy-start.8 = (f32[322,130]{0,1:T(8,128)S(1)}, f32[322,130]{0,1:T(8,128)}, u32[]{:S(2)}) copy-start(f32[322,130]{0,1:T(8,128)} %copy-done.7) | copy-start | bytes 502324
  195.6 9.5 %copy-start.15 = (f32[320,128]{0,1:T(8,128)}, f32[320,128]{0,1:T(8,128)S(1)}, u32[]{:S(2)}) copy-start(f32[320,128]{0,1:T(8,128)S(1)} %get-tuple-element.57) | copy-start | bytes 491524
  195.6 9.5 %copy-start.21 = (f32[320,128]{0,1:T(8,128)}, f32[320,128]{0,1:T(8,128)S(1)}, u32[]{:S(2)}) copy-start(f32[320,128]{0,1:T(8,128)S(1)} %get-tuple-element.58) | copy-start | bytes 491524
  195.7 7.0 %collective-permute-start.16 = (f32[320,1]{0,1:T(1,128)S(1)}, f32[320,1]{0,1:T(1,128)S(1)}, u32[]{:S(2)}, u32[]{:S(2)}) collective-permute-start(f32[320,1]{0,1:T(1,128)S(1)} %get-tuple-element.96), channel_id=1, source_target_pairs={{8,0},{16,8},{24,16},{32,24},{40,32},{48,40},{56,48},{64,56},{72,6... | collective-permute-start | bytes 3848 | tf_op jit(solution)/shard_map/ppermute | solution.py:57
  196.4 6.9 %collective-permute-start.17 = (f32[320,1]{0,1:T(1,128)S(1)}, f32[320,1]{0,1:T(1,128)S(1)}, u32[]{:S(2)}, u32[]{:S(2)}) collective-permute-start(f32[320,1]{0,1:T(1,128)S(1)} %get-tuple-element.95), channel_id=1, source_target_pairs={{0,8},{8,16},{16,24},{24,32},{32,40},{40,48},{48,56},{56,64},{64,7... | collective-permute-start | bytes 3848 | tf_op jit(solution)/shard_map/ppermute | solution.py:56
  197.8 4.9 %collective-permute-start.19 = (f32[1,128]{0,1:T(8,128)S(1)}, f32[1,128]{0,1:T(8,128)S(1)}, u32[]{:S(2)}, u32[]{:S(2)}) collective-permute-start(f32[1,128]{0,1:T(8,128)S(1)} %get-tuple-element.94), channel_id=1, source_target_pairs={{0,1},{1,2},{2,3},{3,4},{4,5},{5,6},{6,7},{7,0},{8,9},{9,10},{10,1... | collective-permute-start | bytes 1544 | tf_op jit(solution)/shard_map/ppermute | solution.py:56
  197.8 4.9 %collective-permute-start.18 = (f32[1,128]{0,1:T(8,128)S(1)}, f32[1,128]{0,1:T(8,128)S(1)}, u32[]{:S(2)}, u32[]{:S(2)}) collective-permute-start(f32[1,128]{0,1:T(8,128)S(1)} %get-tuple-element.93), channel_id=1, source_target_pairs={{1,0},{2,1},{3,2},{4,3},{5,4},{6,5},{7,6},{0,7},{9,8},{10,9},{11,1... | collective-permute-start | bytes 1544 | tf_op jit(solution)/shard_map/ppermute | solution.py:57
  206.3 0.6 copy-start.36
  219.3 1.1 copy-start.37
  236.6 1.1 copy-start.38
  250.0 1.1 copy-start.39
  262.8 9.7 %copy-start.16 = (f32[320,128]{0,1:T(8,128)}, f32[320,128]{0,1:T(8,128)S(1)}, u32[]{:S(2)}) copy-start(f32[320,128]{0,1:T(8,128)S(1)} %get-tuple-element.54) | copy-start | bytes 491524
  262.9 4.9 %collective-permute-start.23 = (f32[1,128]{0,1:T(8,128)S(1)}, f32[1,128]{0,1:T(8,128)S(1)}, u32[]{:S(2)}, u32[]{:S(2)}) collective-permute-start(f32[1,128]{0,1:T(8,128)S(1)} %get-tuple-element.90), channel_id=1, source_target_pairs={{0,1},{1,2},{2,3},{3,4},{4,5},{5,6},{6,7},{7,0},{8,9},{9,10},{10,1... | collective-permute-start | bytes 1544 | tf_op jit(solution)/shard_map/ppermute | solution.py:56
  263.1 6.2 %collective-permute-start.20 = (f32[320,1]{0,1:T(1,128)S(1)}, f32[320,1]{0,1:T(1,128)S(1)}, u32[]{:S(2)}, u32[]{:S(2)}) collective-permute-start(f32[320,1]{0,1:T(1,128)S(1)} %get-tuple-element.92), channel_id=1, source_target_pairs={{8,0},{16,8},{24,16},{32,24},{40,32},{48,40},{56,48},{64,56},{72,6... | collective-permute-start | bytes 3848 | tf_op jit(solution)/shard_map/ppermute | solution.py:57
  263.3 6.9 %collective-permute-start.21 = (f32[320,1]{0,1:T(1,128)S(1)}, f32[320,1]{0,1:T(1,128)S(1)}, u32[]{:S(2)}, u32[]{:S(2)}) collective-permute-start(f32[320,1]{0,1:T(1,128)S(1)} %get-tuple-element.91), channel_id=1, source_target_pairs={{0,8},{8,16},{16,24},{24,32},{32,40},{40,48},{48,56},{56,64},{64,7... | collective-permute-start | bytes 3848 | tf_op jit(solution)/shard_map/ppermute | solution.py:56
  265.1 4.1 %collective-permute-start.22 = (f32[1,128]{0,1:T(8,128)S(1)}, f32[1,128]{0,1:T(8,128)S(1)}, u32[]{:S(2)}, u32[]{:S(2)}) collective-permute-start(f32[1,128]{0,1:T(8,128)S(1)} %get-tuple-element.89), channel_id=1, source_target_pairs={{1,0},{2,1},{3,2},{4,3},{5,4},{6,5},{7,6},{0,7},{9,8},{10,9},{11,1... | collective-permute-start | bytes 1544 | tf_op jit(solution)/shard_map/ppermute | solution.py:57
  331.9 10.6 %collective-permute-start.26 = (f32[1,128]{0,1:T(8,128)}, f32[1,128]{0,1:T(8,128)}, u32[]{:S(2)}, u32[]{:S(2)}) collective-permute-start(f32[1,128]{0,1:T(8,128)} %slice.452), channel_id=1, source_target_pairs={{1,0},{2,1},{3,2},{4,3},{5,4},{6,5},{7,6},{0,7},{9,8},{10,9},{11,1... | collective-permute-start | bytes 1544 | tf_op jit(solution)/shard_map/ppermute | solution.py:57
  332.9 9.6 %collective-permute-start.24 = (f32[320,1]{0,1:T(1,128)}, f32[320,1]{0,1:T(1,128)S(1)}, u32[]{:S(2)}, u32[]{:S(2)}) collective-permute-start(f32[320,1]{0,1:T(1,128)} %get-tuple-element.87), channel_id=1, source_target_pairs={{8,0},{16,8},{24,16},{32,24},{40,32},{48,40},{56,48},{64,56},{72,6... | collective-permute-start | bytes 3848 | tf_op jit(solution)/shard_map/ppermute | solution.py:57
  333.1 9.3 %collective-permute-start.25 = (f32[320,1]{0,1:T(1,128)}, f32[320,1]{0,1:T(1,128)S(1)}, u32[]{:S(2)}, u32[]{:S(2)}) collective-permute-start(f32[320,1]{0,1:T(1,128)} %get-tuple-element.86), channel_id=1, source_target_pairs={{0,8},{8,16},{16,24},{24,32},{32,40},{40,48},{48,56},{56,64},{64,7... | collective-permute-start | bytes 3848 | tf_op jit(solution)/shard_map/ppermute | solution.py:56
  339.3 4.2 %copy-start.10 = (f32[4,322,130]{1,2,0:T(8,128)S(1)}, f32[4,322,130]{1,2,0:T(8,128)}, u32[]{:S(2)}) copy-start(f32[4,322,130]{1,2,0:T(8,128)} %get-tuple-element.66) | copy-start | bytes 2009284
  339.3 4.2 %copy-start.11 = (f32[4,322,130]{1,2,0:T(8,128)S(1)}, f32[4,322,130]{1,2,0:T(8,128)}, u32[]{:S(2)}) copy-start(f32[4,322,130]{1,2,0:T(8,128)} %get-tuple-element.67) | copy-start | bytes 2009284
  (3 other events, 1.6 us)
